TPU v7x, 256 devices: a whole 4x4x8 slice. The times are simulated.
256 devices in a mesh: blk: 64 (over x, y_hi, z), rep: 4 (over y_lo, core).
Axes of the slice: x: 4, y: 4 (y_hi: 2, y_lo: 2; y = y_hi * 2 + y_lo), z: 8, core: 2. Of those that a mesh axis runs over, the one named last changes fastest.
Arguments:
- embeddings: float32 [131072, 768], P(('blk', 'rep')), may hold values from -6 to 6
- ranks: int32 [131072], replicated, may hold values from 0 to 131071, each once
Outputs:
- earlier_best: float32 [131072], P(('blk', 'rep'))
- later_best: float32 [131072], P(('blk', 'rep'))
Inputs may be any that keep to these rules, and one draw needn't show every extreme that they name: ranks is a permutation of 0 .. 131071.
All inputs are finite; a program needn't handle non-finite values.
Results may differ from a plain program's by a relative error of at most 0.0012.
Values may be sent and summed in bfloat16 or wider, within the bound.
No kernel may reach another device: no remote copies, remote signals or barrier semaphores. Data moves between devices by JAX's collectives and lax.ppermute only.
A program may use at most 64 MiB of HBM per device.

v0:
```python
import jax
import jax.numpy as jnp
from jax import lax
from jax.sharding import PartitionSpec as P


AXES = ("blk", "rep")
LINE = 8
LOW = -1.0


def routes(blocks, move):
    pairs = []
    for block in range(blocks):
        for place in range(4):
            target = move(block, place)
            if target is not None:
                pairs.append((4 * block + place, target[0] % blocks * 4 + target[1]))
    return pairs


def onward(block, place):
    return block + 1, place ^ 2 if block % LINE == LINE - 1 else place


def back(block, place):
    return block - 1, place ^ 2 if block % LINE == 0 else place


def back_twice(block, place):
    return back(*back(block, place))


def other(bits):
    return lambda block, place: (block, place ^ bits)


def scores_of(left, right):
    return lax.dot_general(
        left, right, (((1,), (1,)), ((), ())), preferred_element_type=jnp.float32
    )


def best_pair(host, host_rank, visit, visit_rank):
    kept = jnp.where(
        visit_rank[None, :] < host_rank[:, None], scores_of(host, visit), jnp.float32(LOW)
    )
    return jnp.max(kept, axis=1), jnp.max(kept, axis=0)


def both_ways(own, own_rank, peer, peer_rank):
    scores = scores_of(own, peer)
    earlier = jnp.where(peer_rank[None, :] < own_rank[:, None], scores, jnp.float32(LOW))
    later = jnp.where(own_rank[:, None] < peer_rank[None, :], scores, jnp.float32(LOW))
    return jnp.max(earlier, axis=1), jnp.max(later, axis=1)


def largest(values):
    best = values[0]
    for value in values[1:]:
        best = jnp.maximum(best, value)
    return best


def shards(embeddings, ranks):
    rows = embeddings.shape[0]
    blocks = lax.axis_size("blk")
    block = lax.axis_index("blk")
    place = lax.axis_index("rep")
    z = block % LINE

    def send(value, move):
        return lax.ppermute(value, AXES, routes(blocks, move))

    def ranks_of(block_id, place_id):
        start = (block_id * 4 + place_id) * rows
        return lax.dynamic_slice_in_dim(ranks, start, rows)

    squares = jnp.sum(embeddings * embeddings, axis=1, keepdims=True)
    unit = (embeddings * lax.rsqrt(squares + 1e-06)).astype(jnp.bfloat16)

    visit1 = send(unit, onward)
    ahead = send(unit, back)
    across = send(unit, other(2))
    beside = send(unit, other(1))
    visit2 = send(visit1, onward)
    ahead_across = send(ahead, other(2))
    across_beside = send(across, other(1))
    ahead_beside = send(ahead, other(1))
    ahead_both = send(ahead_across, other(1))

    host = [unit, beside, across, across_beside]
    host_ranks = [ranks_of(block, place ^ k) for k in range(4)]
    prev = (block + blocks - 1) % blocks
    prev2 = (block + blocks - 2) % blocks
    nxt = (block + 1) % blocks
    prev_place = jnp.where(z == 0, place ^ 2, place)
    prev2_place = jnp.where(z <= 1, place ^ 2, place)
    next_place = jnp.where(z == LINE - 1, place ^ 2, place)
    rank1 = ranks_of(prev, prev_place)
    rank2 = ranks_of(prev2, prev2_place)
    front = [ahead, ahead_beside, ahead_across, ahead_both]
    front_ranks = [ranks_of(nxt, next_place ^ k) for k in range(4)]

    def tiles(pair, left, left_ranks, right, right_rank):
        out = []
        for k in range(4):
            out.append(pair(left[k], left_ranks[k], right, right_rank))
        return out

    own = []
    for k in range(4):
        own.append(both_ways(unit, host_ranks[0], host[k], host_ranks[k]))
    earlier = largest([pair[0] for pair in own])
    later = largest([pair[1] for pair in own])

    one = tiles(best_pair, host, host_ranks, visit1, rank1)
    two = tiles(best_pair, front, front_ranks, visit1, rank1)
    columns1 = largest([pair[1] for pair in one + two])
    three = tiles(best_pair, front, front_ranks, visit2, rank2)
    columns2 = largest([pair[1] for pair in three])
    front_rows = jnp.stack([jnp.maximum(a[0], b[0]) for a, b in zip(two, three)])
    host_rows = jnp.stack([pair[0] for pair in one])

    merged = jnp.maximum(host_rows, send(front_rows, onward))
    later = jnp.maximum(later, send(columns1, back))
    later = jnp.maximum(later, send(columns2, back_twice))
    earlier = jnp.maximum(earlier, merged[0])
    for k in (2, 3, 1):
        earlier = jnp.maximum(earlier, send(merged[k], other(k)))
    return earlier, later


def solution(mesh):
    return jax.shard_map(
        shards,
        mesh=mesh,
        in_specs=(P(("blk", "rep"), None), P()),
        out_specs=(P(("blk", "rep")), P(("blk", "rep"))),
        check_vma=False,
    )
```

profile of v0, /device:TPU:1, one launch (start us, length us, event | category | flops | bytes accessed | tf_op | source)
XLA Modules:
  0.0 82.9 jit_solution(6792286376072279809)
XLA Ops:
  0.6 0.0 copy-start
  0.6 1.7 %multiply_reduce_fusion = f32[512]{0:T(512)S(1)} fusion(f32[512,768]{1,0:T(8,128)} %param.2), kind=kLoop, calls=%fused_computation.1 | loop fusion | flops 785920 | bytes 1574912 | tf_op jit(solution)/shard_map/reduce_sum | solution.py:79
  2.4 0.2 copy-done
  2.5 0.1 multiply_convert_fusion
  2.7 11.1 %collective-permute-start.4 = (bf16[512,768]{1,0:T(8,128)(2,1)S(1)}, bf16[512,768]{1,0:T(8,128)(2,1)}, u32[]{:S(2)}, u32[]{:S(2)}) collective-permute-start(bf16[512,768]{1,0:T(8,128)(2,1)S(1)} %multiply_convert_fusion), channel_id=1, source_target_pairs={{0,254},{1,255},{2,252},{3,253},{4,0},{5,1},{6,2},{7,3},{8,4},{9,5... | collective-permute-start | bytes 2359304 | tf_op jit(solution)/shard_map/ppermute | solution.py:73
  13.8 0.0 collective-permute-start.3
  13.8 0.0 collective-permute-start.1
  13.8 1.1 %collective-permute-start = (bf16[512,768]{1,0:T(8,128)(2,1)S(1)}, bf16[512,768]{1,0:T(8,128)(2,1)S(1)}, u32[]{:S(2)}, u32[]{:S(2)}) collective-permute-start(bf16[512,768]{1,0:T(8,128)(2,1)S(1)} %multiply_convert_fusion), channel_id=1, source_target_pairs={{0,1},{1,0},{2,3},{3,2},{4,5},{5,4},{6,7},{7,6},{8,9},{9,8},{10,11... | collective-permute-start | bytes 2359304 | tf_op jit(solution)/shard_map/ppermute | solution.py:73
  14.9 0.9 %fusion.12 = (s32[512]{0:T(512)S(1)}, s32[512]{0:T(512)S(1)}, s32[512]{0:T(512)S(1)}, s32[512]{0:T(512)S(1)}, s32[512]{0:T(512)S(1)}, /*index=5*/s32[512]{0:T(51...) fusion(s32[131072]{0:T(1024)} %param.3, s32[]{:T(128)S(6)} %select_n.119, s32[]{:T(128)S(6)} %select_n.143, ...), kind=kLoop, calls=%fused_computation.41 | loop fusion | bytes 41000 | tf_op jit(solution)/shard_map/dynamic_slice | solution.py:77
  15.8 0.6 fusion.14
  16.4 13.6 %collective-permute-done.4 = bf16[512,768]{1,0:T(8,128)(2,1)} collective-permute-done((bf16[512,768]{1,0:T(8,128)(2,1)S(1)}, bf16[512,768]{1,0:T(8,128)(2,1)}, u32[]{:S(2)}, u32[]{:S(2)}) %collective-permute-start.4) | collective-permute-done | bytes 786464 | tf_op jit(solution)/shard_map/ppermute | solution.py:73
  30.0 0.0 collective-permute-start.7
  30.0 1.7 %collective-permute-start.6 = (bf16[512,768]{1,0:T(8,128)(2,1)}, bf16[512,768]{1,0:T(8,128)(2,1)S(1)}, u32[]{:S(2)}, u32[]{:S(2)}) collective-permute-start(bf16[512,768]{1,0:T(8,128)(2,1)} %collective-permute-done.4), channel_id=1, source_target_pairs={{0,1},{1,0},{2,3},{3,2},{4,5},{5,4},{6,7},{7,6},{8,9},{9,8},{10,11... | collective-permute-start | bytes 2359304 | tf_op jit(solution)/shard_map/ppermute | solution.py:73
  31.7 5.7 %collective-permute-done.3 = bf16[512,768]{1,0:T(8,128)(2,1)S(1)} collective-permute-done((bf16[512,768]{1,0:T(8,128)(2,1)S(1)}, bf16[512,768]{1,0:T(8,128)(2,1)S(1)}, u32[]{:S(2)}, u32[]{:S(2)}) %collective-permute-start.3) | collective-permute-done | bytes 786464 | tf_op jit(solution)/shard_map/ppermute | solution.py:73
  37.4 0.0 collective-permute-start.5
  37.4 0.0 collective-permute-done.1
  37.4 1.8 %collective-permute-start.2 = (bf16[512,768]{1,0:T(8,128)(2,1)S(1)}, bf16[512,768]{1,0:T(8,128)(2,1)S(1)}, u32[]{:S(2)}, u32[]{:S(2)}) collective-permute-start(bf16[512,768]{1,0:T(8,128)(2,1)S(1)} %collective-permute-done.1), channel_id=1, source_target_pairs={{0,1},{1,0},{2,3},{3,2},{4,5},{5,4},{6,7},{7,6},{8,9},{9,8},{10,11... | collective-permute-start | bytes 2359304 | tf_op jit(solution)/shard_map/ppermute | solution.py:73
  39.2 0.0 collective-permute-done
  39.2 0.6 fusion.15
  39.8 1.8 %fusion.4 = (f32[512]{0:T(512)S(1)}, f32[512]{0:T(512)S(1)}) fusion(bf16[512,768]{1,0:T(8,128)(2,1)} %collective-permute-done.4, bf16[512,768]{1,0:T(8,128)(2,1)S(1)} %collective-permute-done.3, s32[512]{0:T(512)S(1)} %get-tuple-element.43, s32[512]{0:T(512)S(1)} %get-tuple-element.44), kind=kOutput, calls=%fused_computation.33 | convolution fusion | flops 403700736 | bytes 1581056 | tf_op jit(solution)/shard_map/dot_general | solution.py:39
  41.6 0.7 fusion.2
  42.3 0.7 fusion
  43.0 0.7 fusion.1
  43.7 0.6 fusion.16
  44.3 4.3 %collective-permute-done.7 = bf16[512,768]{1,0:T(8,128)(2,1)S(1)} collective-permute-done((bf16[512,768]{1,0:T(8,128)(2,1)}, bf16[512,768]{1,0:T(8,128)(2,1)S(1)}, u32[]{:S(2)}, u32[]{:S(2)}) %collective-permute-start.7) | collective-permute-done | bytes 786464 | tf_op jit(solution)/shard_map/ppermute | solution.py:73
  48.6 2.0 %collective-permute-start.8 = (bf16[512,768]{1,0:T(8,128)(2,1)S(1)}, bf16[512,768]{1,0:T(8,128)(2,1)S(1)}, u32[]{:S(2)}, u32[]{:S(2)}) collective-permute-start(bf16[512,768]{1,0:T(8,128)(2,1)S(1)} %collective-permute-done.7), channel_id=1, source_target_pairs={{0,1},{1,0},{2,3},{3,2},{4,5},{5,4},{6,7},{7,6},{8,9},{9,8},{10,11... | collective-permute-start | bytes 2359304 | tf_op jit(solution)/shard_map/ppermute | solution.py:73
  50.6 0.7 fusion.6
  51.3 8.8 %collective-permute-done.5 = bf16[512,768]{1,0:T(8,128)(2,1)S(1)} collective-permute-done((bf16[512,768]{1,0:T(8,128)(2,1)S(1)}, bf16[512,768]{1,0:T(8,128)(2,1)S(1)}, u32[]{:S(2)}, u32[]{:S(2)}) %collective-permute-start.5) | collective-permute-done | bytes 786464 | tf_op jit(solution)/shard_map/ppermute | solution.py:73
  60.1 0.7 fusion.10
  60.8 0.0 collective-permute-done.6
  60.8 0.7 fusion.5
  61.5 0.7 fusion.8
  62.2 1.8 %fusion.9 = (f32[512]{0:T(512)S(1)}, f32[512]{0:T(512)S(1)}) fusion(bf16[512,768]{1,0:T(8,128)(2,1)} %collective-permute-done.4, bf16[512,768]{1,0:T(8,128)(2,1)S(1)} %collective-permute-done.5, s32[512]{0:T(512)S(1)} %get-tuple-element.43, s32[512]{0:T(512)S(1)} %get-tuple-element.42), kind=kOutput, calls=%fused_computation.38 | convolution fusion | flops 403700736 | bytes 1581056 | tf_op jit(solution)/shard_map/dot_general | solution.py:39
  64.0 0.0 collective-permute-done.2
  64.0 0.7 fusion.3
  64.7 1.2 %select_reduce_fusion.2 = (f32[512]{0:T(512)S(1)}, f32[512]{0:T(512)S(1)}, f32[512]{0:T(512)S(1)}, f32[512]{0:T(512)S(1)}, f32[512]{0:T(512)S(1)}, /*index=5*/f32[512]{0:T(512)S(1)}, f32[512]{0:T(512)S(1)}, f32[512]{0:T(512)S(1)}) fusion(f32[512,512]{0,1:T(8,128)S(1)} %fusion.15, s32[512]{0:T(512)S(1)} %get-tuple-element.40, s32[512]{0:T(512)S(1)} %get-tuple-element.47, ...), kind=kOutput, calls=%fused_computation.16 | convolution fusion | flops 408940544 | bytes 4743168 | tf_op jit(solution)/shard_map/dot_general | solution.py:39
  66.0 0.0 collective-permute-done.8
  66.0 0.7 fusion.7
  66.7 0.7 fusion.11
  67.4 0.1 collective-permute-start.9
  67.5 0.4 collective-permute-start.14
  67.9 6.5 %collective-permute-start.13 = (f32[512]{0:T(512)S(1)}, f32[512]{0:T(512)S(1)}, u32[]{:S(2)}, u32[]{:S(2)}) collective-permute-start(f32[512]{0:T(512)S(1)} %maximum_maximum_fusion.3), channel_id=1, source_target_pairs={{0,254},{1,255},{2,252},{3,253},{4,0},{5,1},{6,2},{7,3},{8,4},{9,5... | collective-permute-start | bytes 6152 | tf_op jit(solution)/shard_map/ppermute | solution.py:73
  74.5 0.9 %collective-permute-done.9 = f32[4,512]{1,0:T(4,128)S(1)} collective-permute-done((f32[4,512]{1,0:T(4,128)S(1)}, f32[4,512]{1,0:T(4,128)S(1)}, u32[]{:S(2)}, u32[]{:S(2)}) %collective-permute-start.9) | collective-permute-done | bytes 8224 | tf_op jit(solution)/shard_map/ppermute | solution.py:73
  75.4 3.9 %collective-permute-start.12 = (f32[512]{0:T(512)S(1)}, f32[512]{0:T(512)S(1)}, u32[]{:S(2)}, u32[]{:S(2)}) collective-permute-start(f32[512]{0:T(512)S(1)} %bitcast.55), channel_id=1, source_target_pairs={{0,1},{1,0},{2,3},{3,2},{4,5},{5,4},{6,7},{7,6},{8,9},{9,8},{10,11... | collective-permute-start | bytes 6152 | tf_op jit(solution)/shard_map/ppermute | solution.py:73
  79.3 0.0 collective-permute-start.11
  79.3 1.4 %collective-permute-start.10 = (f32[512]{0:T(512)S(1)}, f32[512]{0:T(512)S(1)}, u32[]{:S(2)}, u32[]{:S(2)}) collective-permute-start(f32[512]{0:T(512)S(1)} %bitcast.53), channel_id=1, source_target_pairs={{0,2},{1,3},{2,0},{3,1},{4,6},{5,7},{6,4},{7,5},{8,10},{9,11},{10,... | collective-permute-start | bytes 6152 | tf_op jit(solution)/shard_map/ppermute | solution.py:73
  80.8 0.0 collective-permute-done.14
  80.8 0.0 collective-permute-done.13
  80.8 0.6 maximum_maximum_fusion.2
  81.4 0.0 collective-permute-done.12
  81.4 1.0 %collective-permute-done.11 = f32[512]{0:T(512)S(1)} collective-permute-done((f32[512]{0:T(512)S(1)}, f32[512]{0:T(512)S(1)}, u32[]{:S(2)}, u32[]{:S(2)}) %collective-permute-start.11) | collective-permute-done | bytes 2080 | tf_op jit(solution)/shard_map/ppermute | solution.py:73
  82.3 0.0 collective-permute-done.10
  82.4 0.6 maximum_maximum_fusion.4
  (10 shorter events, 0.1 us)
Async XLA Ops:
  0.6 1.9 %copy-start = (f32[512,768]{1,0:T(8,128)S(1)}, f32[512,768]{1,0:T(8,128)}, u32[]{:S(2)}) copy-start(f32[512,768]{1,0:T(8,128)} %param.2) | copy-start | bytes 4718596
  2.7 27.3 %collective-permute-start.4 = (bf16[512,768]{1,0:T(8,128)(2,1)S(1)}, bf16[512,768]{1,0:T(8,128)(2,1)}, u32[]{:S(2)}, u32[]{:S(2)}) collective-permute-start(bf16[512,768]{1,0:T(8,128)(2,1)S(1)} %multiply_convert_fusion), channel_id=1, source_target_pairs={{0,254},{1,255},{2,252},{3,253},{4,0},{5,1},{6,2},{7,3},{8,4},{9,5... | collective-permute-start | bytes 2359304 | tf_op jit(solution)/shard_map/ppermute | solution.py:73
  13.8 23.6 %collective-permute-start.3 = (bf16[512,768]{1,0:T(8,128)(2,1)S(1)}, bf16[512,768]{1,0:T(8,128)(2,1)S(1)}, u32[]{:S(2)}, u32[]{:S(2)}) collective-permute-start(bf16[512,768]{1,0:T(8,128)(2,1)S(1)} %multiply_convert_fusion), channel_id=1, source_target_pairs={{0,4},{1,5},{2,6},{3,7},{4,8},{5,9},{6,10},{7,11},{8,12},{9,13},{1... | collective-permute-start | bytes 2359304 | tf_op jit(solution)/shard_map/ppermute | solution.py:73
  13.8 23.6 %collective-permute-start.1 = (bf16[512,768]{1,0:T(8,128)(2,1)S(1)}, bf16[512,768]{1,0:T(8,128)(2,1)S(1)}, u32[]{:S(2)}, u32[]{:S(2)}) collective-permute-start(bf16[512,768]{1,0:T(8,128)(2,1)S(1)} %multiply_convert_fusion), channel_id=1, source_target_pairs={{0,2},{1,3},{2,0},{3,1},{4,6},{5,7},{6,4},{7,5},{8,10},{9,11},{10,... | collective-permute-start | bytes 2359304 | tf_op jit(solution)/shard_map/ppermute | solution.py:73
  13.8 25.4 %collective-permute-start = (bf16[512,768]{1,0:T(8,128)(2,1)S(1)}, bf16[512,768]{1,0:T(8,128)(2,1)S(1)}, u32[]{:S(2)}, u32[]{:S(2)}) collective-permute-start(bf16[512,768]{1,0:T(8,128)(2,1)S(1)} %multiply_convert_fusion), channel_id=1, source_target_pairs={{0,1},{1,0},{2,3},{3,2},{4,5},{5,4},{6,7},{7,6},{8,9},{9,8},{10,11... | collective-permute-start | bytes 2359304 | tf_op jit(solution)/shard_map/ppermute | solution.py:73
  30.0 18.6 %collective-permute-start.7 = (bf16[512,768]{1,0:T(8,128)(2,1)}, bf16[512,768]{1,0:T(8,128)(2,1)S(1)}, u32[]{:S(2)}, u32[]{:S(2)}) collective-permute-start(bf16[512,768]{1,0:T(8,128)(2,1)} %collective-permute-done.4), channel_id=1, source_target_pairs={{0,2},{1,3},{2,0},{3,1},{4,6},{5,7},{6,4},{7,5},{8,10},{9,11},{10,... | collective-permute-start | bytes 2359304 | tf_op jit(solution)/shard_map/ppermute | solution.py:73
  30.0 30.8 %collective-permute-start.6 = (bf16[512,768]{1,0:T(8,128)(2,1)}, bf16[512,768]{1,0:T(8,128)(2,1)S(1)}, u32[]{:S(2)}, u32[]{:S(2)}) collective-permute-start(bf16[512,768]{1,0:T(8,128)(2,1)} %collective-permute-done.4), channel_id=1, source_target_pairs={{0,1},{1,0},{2,3},{3,2},{4,5},{5,4},{6,7},{7,6},{8,9},{9,8},{10,11... | collective-permute-start | bytes 2359304 | tf_op jit(solution)/shard_map/ppermute | solution.py:73
  37.4 22.7 %collective-permute-start.5 = (bf16[512,768]{1,0:T(8,128)(2,1)S(1)}, bf16[512,768]{1,0:T(8,128)(2,1)S(1)}, u32[]{:S(2)}, u32[]{:S(2)}) collective-permute-start(bf16[512,768]{1,0:T(8,128)(2,1)S(1)} %collective-permute-done.3), channel_id=1, source_target_pairs={{0,4},{1,5},{2,6},{3,7},{4,8},{5,9},{6,10},{7,11},{8,12},{9,13},{1... | collective-permute-start | bytes 2359304 | tf_op jit(solution)/shard_map/ppermute | solution.py:73
  37.4 26.6 %collective-permute-start.2 = (bf16[512,768]{1,0:T(8,128)(2,1)S(1)}, bf16[512,768]{1,0:T(8,128)(2,1)S(1)}, u32[]{:S(2)}, u32[]{:S(2)}) collective-permute-start(bf16[512,768]{1,0:T(8,128)(2,1)S(1)} %collective-permute-done.1), channel_id=1, source_target_pairs={{0,1},{1,0},{2,3},{3,2},{4,5},{5,4},{6,7},{7,6},{8,9},{9,8},{10,11... | collective-permute-start | bytes 2359304 | tf_op jit(solution)/shard_map/ppermute | solution.py:73
  48.6 17.3 %collective-permute-start.8 = (bf16[512,768]{1,0:T(8,128)(2,1)S(1)}, bf16[512,768]{1,0:T(8,128)(2,1)S(1)}, u32[]{:S(2)}, u32[]{:S(2)}) collective-permute-start(bf16[512,768]{1,0:T(8,128)(2,1)S(1)} %collective-permute-done.7), channel_id=1, source_target_pairs={{0,1},{1,0},{2,3},{3,2},{4,5},{5,4},{6,7},{7,6},{8,9},{9,8},{10,11... | collective-permute-start | bytes 2359304 | tf_op jit(solution)/shard_map/ppermute | solution.py:73
  67.4 8.0 %collective-permute-start.9 = (f32[4,512]{1,0:T(4,128)S(1)}, f32[4,512]{1,0:T(4,128)S(1)}, u32[]{:S(2)}, u32[]{:S(2)}) collective-permute-start(f32[4,512]{1,0:T(4,128)S(1)} %pad_maximum_fusion), channel_id=1, source_target_pairs={{0,4},{1,5},{2,6},{3,7},{4,8},{5,9},{6,10},{7,11},{8,12},{9,13},{1... | collective-permute-start | bytes 24584 | tf_op jit(solution)/shard_map/ppermute | solution.py:73
  67.5 13.3 %collective-permute-start.14 = (f32[512]{0:T(512)S(1)}, f32[512]{0:T(512)S(1)}, u32[]{:S(2)}, u32[]{:S(2)}) collective-permute-start(f32[512]{0:T(512)S(1)} %maximum_maximum_fusion.1), channel_id=1, source_target_pairs={{0,250},{1,251},{2,248},{3,249},{4,254},{5,255},{6,252},{7,253},{8... | collective-permute-start | bytes 6152 | tf_op jit(solution)/shard_map/ppermute | solution.py:73
  67.9 12.9 %collective-permute-start.13 = (f32[512]{0:T(512)S(1)}, f32[512]{0:T(512)S(1)}, u32[]{:S(2)}, u32[]{:S(2)}) collective-permute-start(f32[512]{0:T(512)S(1)} %maximum_maximum_fusion.3), channel_id=1, source_target_pairs={{0,254},{1,255},{2,252},{3,253},{4,0},{5,1},{6,2},{7,3},{8,4},{9,5... | collective-permute-start | bytes 6152 | tf_op jit(solution)/shard_map/ppermute | solution.py:73
  75.4 6.0 %collective-permute-start.12 = (f32[512]{0:T(512)S(1)}, f32[512]{0:T(512)S(1)}, u32[]{:S(2)}, u32[]{:S(2)}) collective-permute-start(f32[512]{0:T(512)S(1)} %bitcast.55), channel_id=1, source_target_pairs={{0,1},{1,0},{2,3},{3,2},{4,5},{5,4},{6,7},{7,6},{8,9},{9,8},{10,11... | collective-permute-start | bytes 6152 | tf_op jit(solution)/shard_map/ppermute | solution.py:73
  79.3 3.0 %collective-permute-start.11 = (f32[512]{0:T(512)S(1)}, f32[512]{0:T(512)S(1)}, u32[]{:S(2)}, u32[]{:S(2)}) collective-permute-start(f32[512]{0:T(512)S(1)} %bitcast.54), channel_id=1, source_target_pairs={{0,3},{1,2},{2,1},{3,0},{4,7},{5,6},{6,5},{7,4},{8,11},{9,10},{10,... | collective-permute-start | bytes 6152 | tf_op jit(solution)/shard_map/ppermute | solution.py:73
  79.3 3.0 %collective-permute-start.10 = (f32[512]{0:T(512)S(1)}, f32[512]{0:T(512)S(1)}, u32[]{:S(2)}, u32[]{:S(2)}) collective-permute-start(f32[512]{0:T(512)S(1)} %bitcast.53), channel_id=1, source_target_pairs={{0,2},{1,3},{2,0},{3,1},{4,6},{5,7},{6,4},{7,5},{8,10},{9,11},{10,... | collective-permute-start | bytes 6152 | tf_op jit(solution)/shard_map/ppermute | solution.py:73
where the time goes:
time: 83.1 us; the launch traced here: 82.9 us
  waiting for transfers between devices  34.4 us (41%)
  starting transfers between devices  30.1 us (36%)
  matrix products  13.6 us (16%)
  other arithmetic  3.09 us (4%)
  local copies, waits for them, and re-layouts  1.08 us (1%)
    ppermute x15, waiting for transfers between devices, send(): return lax.ppermute(value, AXES, routes(blocks, move))  34.4 us
    ppermute x15, starting transfers between devices, send(): return lax.ppermute(value, AXES, routes(blocks, move))  30.1 us
    dot_general x16, matrix products, scores_of(): lax.dot_general(left, right, (((1,), (1,)), ((), ())), preferred_element_...  13.6 us
    reduce_sum x1, other arithmetic, shards(): squares = jnp.sum(embeddings * embeddings, axis=1, keepdims=True)  1.7 us
  transfers between devices with their start and end apart: 15, of which 6 were waited for; matrix products, arithmetic and copies ran while one was open for 17% of the time, Pallas kernels for 0%

commit v1 on v0

--- a/solution.py
+++ b/solution.py
@@ -48,11 +48,14 @@
     return jnp.max(kept, axis=1), jnp.max(kept, axis=0)
 
 
-def both_ways(own, own_rank, peer, peer_rank):
-    scores = scores_of(own, peer)
-    earlier = jnp.where(peer_rank[None, :] < own_rank[:, None], scores, jnp.float32(LOW))
-    later = jnp.where(own_rank[:, None] < peer_rank[None, :], scores, jnp.float32(LOW))
-    return jnp.max(earlier, axis=1), jnp.max(later, axis=1)
+def own_pair(own, own_rank, peer, peer_rank):
+    earlier = jnp.where(
+        peer_rank[None, :] < own_rank[:, None], scores_of(own, peer), jnp.float32(LOW)
+    )
+    later = jnp.where(
+        own_rank[None, :] < peer_rank[:, None], scores_of(peer, own), jnp.float32(LOW)
+    )
+    return jnp.max(earlier, axis=1), jnp.max(later, axis=0)
 
 
 def largest(values):
@@ -79,13 +82,20 @@
     squares = jnp.sum(embeddings * embeddings, axis=1, keepdims=True)
     unit = (embeddings * lax.rsqrt(squares + 1e-06)).astype(jnp.bfloat16)
 
-    visit1 = send(unit, onward)
-    ahead = send(unit, back)
+    def pieces(values, move):
+        return [send(value, move) for value in values]
+
+    ups = pieces(jnp.split(unit, [256]), onward)
+    downs = pieces(jnp.split(unit, [256]), back)
     across = send(unit, other(2))
     beside = send(unit, other(1))
-    visit2 = send(visit1, onward)
-    ahead_across = send(ahead, other(2))
+    upps = pieces(ups, onward)
+    downs_across = pieces(downs, other(2))
     across_beside = send(across, other(1))
+    visit1 = jnp.concatenate(ups)
+    ahead = jnp.concatenate(downs)
+    visit2 = jnp.concatenate(upps)
+    ahead_across = jnp.concatenate(downs_across)
     ahead_beside = send(ahead, other(1))
     ahead_both = send(ahead_across, other(1))
 
@@ -110,7 +120,7 @@
 
     own = []
     for k in range(4):
-        own.append(both_ways(unit, host_ranks[0], host[k], host_ranks[k]))
+        own.append(own_pair(unit, host_ranks[0], host[k], host_ranks[k]))
     earlier = largest([pair[0] for pair in own])
     later = largest([pair[1] for pair in own])
 

time: 83.1 us -> 103 us (1.24)
  starting transfers between devices: 30.1 us -> 41.2 us
  waiting for transfers between devices: 34.4 us -> 39.8 us
  matrix products: 13.6 us -> 16.3 us
    ppermute x15 -> x19, starting transfers between devices: 30.1 us -> 41.2 us  [send(): return lax.ppermute(value, AXES, routes(blocks, move))]
    ppermute x15 -> x19, waiting for transfers between devices: 34.4 us -> 39.8 us  [send(): return lax.ppermute(value, AXES, routes(blocks, move))]
    dot_general x16 -> x19, matrix products: 13.6 us -> 16.3 us  [scores_of(): lax.dot_general(left, right, (((1,), (1,)), ((), ())), preferred_element_...]
  transfers between devices with their start and end apart: 15 -> 19, of which waited for: 6 -> 6; matrix products, arithmetic and copies ran while one was open for 17% -> 18% of each run, Pallas kernels for 0% -> 0%
where the time goes in v1:
time: 103 us; the launch traced here: 102 us
  starting transfers between devices  41.2 us (40%)
  waiting for transfers between devices  39.8 us (39%)
  matrix products  16.3 us (16%)
  other arithmetic  3.1 us (3%)
  local copies, waits for them, and re-layouts  1.35 us (1%)
    ppermute x19, starting transfers between devices, send(): return lax.ppermute(value, AXES, routes(blocks, move))  41.2 us
    ppermute x19, waiting for transfers between devices, send(): return lax.ppermute(value, AXES, routes(blocks, move))  39.8 us
    dot_general x19, matrix products, scores_of(): lax.dot_general(left, right, (((1,), (1,)), ((), ())), preferred_element_...  16.3 us
  transfers between devices with their start and end apart: 19, of which 6 were waited for; matrix products, arithmetic and copies ran while one was open for 18% of the time, Pallas kernels for 0%

profile of v1, /device:TPU:1, one launch (start us, length us, event | category | flops | bytes accessed | tf_op | source)
XLA Modules:
  0.0 102.5 jit_solution(11707738926267699808)
XLA Ops:
  0.6 1.7 %multiply_reduce_fusion = f32[512]{0:T(512)S(1)} fusion(f32[512,768]{1,0:T(8,128)} %param.2), kind=kLoop, calls=%fused_computation.1 | loop fusion | flops 785920 | bytes 1574912 | tf_op jit(solution)/shard_map/reduce_sum | solution.py:82
  2.4 0.2 copy-done
  2.5 0.1 multiply_convert_fusion
  2.7 0.1 fusion.19
  2.7 11.1 %collective-permute-start.5 = (bf16[256,768]{1,0:T(8,128)(2,1)S(1)}, bf16[256,768]{1,0:T(8,128)(2,1)S(1)}, u32[]{:S(2)}, u32[]{:S(2)}) collective-permute-start(bf16[256,768]{1,0:T(8,128)(2,1)S(1)} %get-tuple-element.29), channel_id=1, source_target_pairs={{0,254},{1,255},{2,252},{3,253},{4,0},{5,1},{6,2},{7,3},{8,4},{9,5... | collective-permute-start | bytes 1179656 | tf_op jit(solution)/shard_map/ppermute | solution.py:76
  13.8 0.7 collective-permute-start.6
  14.6 0.7 collective-permute-start.4
  15.3 0.0 collective-permute-start.3
  15.3 0.0 collective-permute-start.1
  15.3 0.9 fusion.20
  16.2 0.7 fusion.6
  16.9 4.7 %collective-permute-done.5 = bf16[256,768]{1,0:T(8,128)(2,1)S(1)} collective-permute-done((bf16[256,768]{1,0:T(8,128)(2,1)S(1)}, bf16[256,768]{1,0:T(8,128)(2,1)S(1)}, u32[]{:S(2)}, u32[]{:S(2)}) %collective-permute-start.5) | collective-permute-done | bytes 393248 | tf_op jit(solution)/shard_map/ppermute | solution.py:76
  21.6 2.7 %collective-permute-start = (bf16[512,768]{1,0:T(8,128)(2,1)S(1)}, bf16[512,768]{1,0:T(8,128)(2,1)S(1)}, u32[]{:S(2)}, u32[]{:S(2)}) collective-permute-start(bf16[512,768]{1,0:T(8,128)(2,1)S(1)} %multiply_convert_fusion), channel_id=1, source_target_pairs={{0,1},{1,0},{2,3},{3,2},{4,5},{5,4},{6,7},{7,6},{8,9},{9,8},{10,11... | collective-permute-start | bytes 2359304 | tf_op jit(solution)/shard_map/ppermute | solution.py:76
  24.3 5.7 %collective-permute-done.6 = bf16[256,768]{1,0:T(8,128)(2,1)S(1)} collective-permute-done((bf16[256,768]{1,0:T(8,128)(2,1)S(1)}, bf16[256,768]{1,0:T(8,128)(2,1)S(1)}, u32[]{:S(2)}, u32[]{:S(2)}) %collective-permute-start.6) | collective-permute-done | bytes 393248 | tf_op jit(solution)/shard_map/ppermute | solution.py:76
  30.1 1.6 %collective-permute-start.9 = (bf16[512,768]{1,0:T(8,128)(2,1)S(1)}, bf16[512,768]{1,0:T(8,128)(2,1)S(1)}, u32[]{:S(2)}, u32[]{:S(2)}) collective-permute-start(bf16[512,768]{1,0:T(8,128)(2,1)S(1)} %constant_dynamic-update-slice_fusion.2), channel_id=1, source_target_pairs={{0,1},{1,0},{2,3},{3,2},{4,5},{5,4},{6,7},{7,6},{8,9},{9,8},{10,11... | collective-permute-start | bytes 2359304 | tf_op jit(solution)/shard_map/ppermute | solution.py:76
  31.7 6.1 %collective-permute-done.3 = bf16[256,768]{1,0:T(8,128)(2,1)S(1)} collective-permute-done((bf16[256,768]{1,0:T(8,128)(2,1)S(1)}, bf16[256,768]{1,0:T(8,128)(2,1)S(1)}, u32[]{:S(2)}, u32[]{:S(2)}) %collective-permute-start.3) | collective-permute-done | bytes 393248 | tf_op jit(solution)/shard_map/ppermute | solution.py:76
  37.9 0.0 collective-permute-start.11
  37.9 0.0 collective-permute-done.4
  37.9 1.5 %collective-permute-start.10 = (bf16[256,768]{1,0:T(8,128)(2,1)S(1)}, bf16[256,768]{1,0:T(8,128)(2,1)S(1)}, u32[]{:S(2)}, u32[]{:S(2)}) collective-permute-start(bf16[256,768]{1,0:T(8,128)(2,1)S(1)} %collective-permute-done.5), channel_id=1, source_target_pairs={{0,2},{1,3},{2,0},{3,1},{4,6},{5,7},{6,4},{7,5},{8,10},{9,11},{10,... | collective-permute-start | bytes 1179656 | tf_op jit(solution)/shard_map/ppermute | solution.py:76
  39.5 0.7 fusion.8
  40.2 0.7 fusion.11
  40.9 14.0 %collective-permute-done.10 = bf16[256,768]{1,0:T(8,128)(2,1)S(1)} collective-permute-done((bf16[256,768]{1,0:T(8,128)(2,1)S(1)}, bf16[256,768]{1,0:T(8,128)(2,1)S(1)}, u32[]{:S(2)}, u32[]{:S(2)}) %collective-permute-start.10) | collective-permute-done | bytes 393248 | tf_op jit(solution)/shard_map/ppermute | solution.py:76
  54.9 0.0 collective-permute-start.7
  54.9 0.0 collective-permute-done.11
  54.9 0.1 collective-permute-start.8
  55.0 0.0 collective-permute-done.1
  55.0 3.0 %collective-permute-start.12 = (bf16[512,768]{1,0:T(8,128)(2,1)S(1)}, bf16[512,768]{1,0:T(8,128)(2,1)S(1)}, u32[]{:S(2)}, u32[]{:S(2)}) collective-permute-start(bf16[512,768]{1,0:T(8,128)(2,1)S(1)} %constant_dynamic-update-slice_fusion.6), channel_id=1, source_target_pairs={{0,1},{1,0},{2,3},{3,2},{4,5},{5,4},{6,7},{7,6},{8,9},{9,8},{10,11... | collective-permute-start | bytes 2359304 | tf_op jit(solution)/shard_map/ppermute | solution.py:76
  58.1 1.7 %fusion.4 = f32[512]{0:T(512)S(1)} fusion(bf16[512,768]{1,0:T(8,128)(2,1)} %collective-permute-done.1, bf16[512,768]{1,0:T(8,128)(2,1)S(1)} %multiply_convert_fusion, s32[512]{0:T(512)S(1)} %get-tuple-element.30, s32[512]{0:T(512)S(1)} %get-tuple-element.36), kind=kOutput, calls=%fused_computation.25 | convolution fusion | flops 403439104 | bytes 1579008 | tf_op jit(solution)/shard_map/dot_general | solution.py:39
  59.8 8.2 %collective-permute-done.7 = bf16[256,768]{1,0:T(8,128)(2,1)S(1)} collective-permute-done((bf16[256,768]{1,0:T(8,128)(2,1)S(1)}, bf16[256,768]{1,0:T(8,128)(2,1)S(1)}, u32[]{:S(2)}, u32[]{:S(2)}) %collective-permute-start.7) | collective-permute-done | bytes 393248 | tf_op jit(solution)/shard_map/ppermute | solution.py:76
  68.0 7.2 %collective-permute-start.2 = (bf16[512,768]{1,0:T(8,128)(2,1)}, bf16[512,768]{1,0:T(8,128)(2,1)S(1)}, u32[]{:S(2)}, u32[]{:S(2)}) collective-permute-start(bf16[512,768]{1,0:T(8,128)(2,1)} %collective-permute-done.1), channel_id=1, source_target_pairs={{0,1},{1,0},{2,3},{3,2},{4,5},{5,4},{6,7},{7,6},{8,9},{9,8},{10,11... | collective-permute-start | bytes 2359304 | tf_op jit(solution)/shard_map/ppermute | solution.py:76
  75.3 1.8 %fusion.1 = f32[512]{0:T(512)S(1)} fusion(bf16[512,768]{1,0:T(8,128)(2,1)S(1)} %multiply_convert_fusion, bf16[512,768]{1,0:T(8,128)(2,1)} %collective-permute-done.1, s32[512]{0:T(512)S(1)} %get-tuple-element.36, s32[512]{0:T(512)S(1)} %get-tuple-element.30), kind=kOutput, calls=%fused_computation.22 | convolution fusion | flops 403439104 | bytes 1579008 | tf_op jit(solution)/shard_map/dot_general | solution.py:39
  77.1 0.0 collective-permute-done.8
  77.1 0.7 fusion.13
  77.8 0.7 fusion.17
  78.5 0.7 fusion.16
  79.2 0.0 collective-permute-done
  79.2 0.6 fusion.3
  79.8 1.8 %fusion.9 = (f32[512]{0:T(512)S(1)}, f32[512]{0:T(512)S(1)}) fusion(bf16[512,768]{1,0:T(8,128)(2,1)} %collective-permute-done.1, bf16[512,768]{1,0:T(8,128)(2,1)S(1)} %constant_dynamic-update-slice_fusion, s32[512]{0:T(512)S(1)} %get-tuple-element.36, s32[512]{0:T(512)S(1)} %get-tuple-element.34), kind=kOutput, calls=%fused_computation.45 | convolution fusion | flops 403700736 | bytes 1581056 | tf_op jit(solution)/shard_map/dot_general | solution.py:39
  81.6 0.7 fusion
  82.4 0.7 fusion.7
  83.0 0.0 collective-permute-done.9
  83.1 0.7 fusion.15
  83.7 0.7 fusion.12
  84.4 0.0 collective-permute-done.12
  84.5 0.7 fusion.18
  85.2 0.1 collective-permute-start.18
  85.2 0.7 fusion.14
  86.0 0.6 collective-permute-start.13
  86.6 0.0 collective-permute-done.2
  86.6 0.7 fusion.10
  87.3 6.4 %collective-permute-start.17 = (f32[512]{0:T(512)S(1)}, f32[512]{0:T(512)S(1)}, u32[]{:S(2)}, u32[]{:S(2)}) collective-permute-start(f32[512]{0:T(512)S(1)} %maximum_maximum_fusion.3), channel_id=1, source_target_pairs={{0,254},{1,255},{2,252},{3,253},{4,0},{5,1},{6,2},{7,3},{8,4},{9,5... | collective-permute-start | bytes 6152 | tf_op jit(solution)/shard_map/ppermute | solution.py:76
  93.7 0.6 fusion.5
  94.3 0.7 fusion.2
  95.0 0.0 collective-permute-done.13
  95.1 3.8 %collective-permute-start.16 = (f32[512]{0:T(512)S(1)}, f32[512]{0:T(512)S(1)}, u32[]{:S(2)}, u32[]{:S(2)}) collective-permute-start(f32[512]{0:T(512)S(1)} %bitcast.61), channel_id=1, source_target_pairs={{0,1},{1,0},{2,3},{3,2},{4,5},{5,4},{6,7},{7,6},{8,9},{9,8},{10,11... | collective-permute-start | bytes 6152 | tf_op jit(solution)/shard_map/ppermute | solution.py:76
  98.9 0.0 collective-permute-start.15
  98.9 1.4 %collective-permute-start.14 = (f32[512]{0:T(512)S(1)}, f32[512]{0:T(512)S(1)}, u32[]{:S(2)}, u32[]{:S(2)}) collective-permute-start(f32[512]{0:T(512)S(1)} %bitcast.59), channel_id=1, source_target_pairs={{0,2},{1,3},{2,0},{3,1},{4,6},{5,7},{6,4},{7,5},{8,10},{9,11},{10,... | collective-permute-start | bytes 6152 | tf_op jit(solution)/shard_map/ppermute | solution.py:76
  100.3 0.0 collective-permute-done.18
  100.3 0.0 collective-permute-done.17
  100.3 0.6 maximum_maximum_fusion.2
  100.9 0.0 collective-permute-done.16
  100.9 1.0 collective-permute-done.15
  101.9 0.0 collective-permute-done.14
  101.9 0.6 maximum_maximum_fusion.4
  (19 shorter events, 0.3 us)
Async XLA Ops:
  0.6 1.9 %copy-start = (f32[512,768]{1,0:T(8,128)S(1)}, f32[512,768]{1,0:T(8,128)}, u32[]{:S(2)}) copy-start(f32[512,768]{1,0:T(8,128)} %param.2) | copy-start | bytes 4718596
  2.7 18.9 %collective-permute-start.5 = (bf16[256,768]{1,0:T(8,128)(2,1)S(1)}, bf16[256,768]{1,0:T(8,128)(2,1)S(1)}, u32[]{:S(2)}, u32[]{:S(2)}) collective-permute-start(bf16[256,768]{1,0:T(8,128)(2,1)S(1)} %get-tuple-element.29), channel_id=1, source_target_pairs={{0,254},{1,255},{2,252},{3,253},{4,0},{5,1},{6,2},{7,3},{8,4},{9,5... | collective-permute-start | bytes 1179656 | tf_op jit(solution)/shard_map/ppermute | solution.py:76
  13.8 16.2 %collective-permute-start.6 = (bf16[256,768]{1,0:T(8,128)(2,1)S(1)}, bf16[256,768]{1,0:T(8,128)(2,1)S(1)}, u32[]{:S(2)}, u32[]{:S(2)}) collective-permute-start(bf16[256,768]{1,0:T(8,128)(2,1)S(1)} %get-tuple-element.28), channel_id=1, source_target_pairs={{0,254},{1,255},{2,252},{3,253},{4,0},{5,1},{6,2},{7,3},{8,4},{9,5... | collective-permute-start | bytes 1179656 | tf_op jit(solution)/shard_map/ppermute | solution.py:76
  14.6 23.3 %collective-permute-start.4 = (bf16[256,768]{1,0:T(8,128)(2,1)S(1)}, bf16[256,768]{1,0:T(8,128)(2,1)S(1)}, u32[]{:S(2)}, u32[]{:S(2)}) collective-permute-start(bf16[256,768]{1,0:T(8,128)(2,1)S(1)} %get-tuple-element.28), channel_id=1, source_target_pairs={{0,4},{1,5},{2,6},{3,7},{4,8},{5,9},{6,10},{7,11},{8,12},{9,13},{1... | collective-permute-start | bytes 1179656 | tf_op jit(solution)/shard_map/ppermute | solution.py:76
  15.3 22.6 %collective-permute-start.3 = (bf16[256,768]{1,0:T(8,128)(2,1)S(1)}, bf16[256,768]{1,0:T(8,128)(2,1)S(1)}, u32[]{:S(2)}, u32[]{:S(2)}) collective-permute-start(bf16[256,768]{1,0:T(8,128)(2,1)S(1)} %get-tuple-element.29), channel_id=1, source_target_pairs={{0,4},{1,5},{2,6},{3,7},{4,8},{5,9},{6,10},{7,11},{8,12},{9,13},{1... | collective-permute-start | bytes 1179656 | tf_op jit(solution)/shard_map/ppermute | solution.py:76
  15.3 39.7 %collective-permute-start.1 = (bf16[512,768]{1,0:T(8,128)(2,1)S(1)}, bf16[512,768]{1,0:T(8,128)(2,1)}, u32[]{:S(2)}, u32[]{:S(2)}) collective-permute-start(bf16[512,768]{1,0:T(8,128)(2,1)S(1)} %multiply_convert_fusion), channel_id=1, source_target_pairs={{0,2},{1,3},{2,0},{3,1},{4,6},{5,7},{6,4},{7,5},{8,10},{9,11},{10,... | collective-permute-start | bytes 2359304 | tf_op jit(solution)/shard_map/ppermute | solution.py:76
  21.6 57.6 %collective-permute-start = (bf16[512,768]{1,0:T(8,128)(2,1)S(1)}, bf16[512,768]{1,0:T(8,128)(2,1)S(1)}, u32[]{:S(2)}, u32[]{:S(2)}) collective-permute-start(bf16[512,768]{1,0:T(8,128)(2,1)S(1)} %multiply_convert_fusion), channel_id=1, source_target_pairs={{0,1},{1,0},{2,3},{3,2},{4,5},{5,4},{6,7},{7,6},{8,9},{9,8},{10,11... | collective-permute-start | bytes 2359304 | tf_op jit(solution)/shard_map/ppermute | solution.py:76
  30.1 53.0 %collective-permute-start.9 = (bf16[512,768]{1,0:T(8,128)(2,1)S(1)}, bf16[512,768]{1,0:T(8,128)(2,1)S(1)}, u32[]{:S(2)}, u32[]{:S(2)}) collective-permute-start(bf16[512,768]{1,0:T(8,128)(2,1)S(1)} %constant_dynamic-update-slice_fusion.2), channel_id=1, source_target_pairs={{0,1},{1,0},{2,3},{3,2},{4,5},{5,4},{6,7},{7,6},{8,9},{9,8},{10,11... | collective-permute-start | bytes 2359304 | tf_op jit(solution)/shard_map/ppermute | solution.py:76
  37.9 17.0 %collective-permute-start.11 = (bf16[256,768]{1,0:T(8,128)(2,1)S(1)}, bf16[256,768]{1,0:T(8,128)(2,1)S(1)}, u32[]{:S(2)}, u32[]{:S(2)}) collective-permute-start(bf16[256,768]{1,0:T(8,128)(2,1)S(1)} %collective-permute-done.6), channel_id=1, source_target_pairs={{0,2},{1,3},{2,0},{3,1},{4,6},{5,7},{6,4},{7,5},{8,10},{9,11},{10,... | collective-permute-start | bytes 1179656 | tf_op jit(solution)/shard_map/ppermute | solution.py:76
  37.9 17.0 %collective-permute-start.10 = (bf16[256,768]{1,0:T(8,128)(2,1)S(1)}, bf16[256,768]{1,0:T(8,128)(2,1)S(1)}, u32[]{:S(2)}, u32[]{:S(2)}) collective-permute-start(bf16[256,768]{1,0:T(8,128)(2,1)S(1)} %collective-permute-done.5), channel_id=1, source_target_pairs={{0,2},{1,3},{2,0},{3,1},{4,6},{5,7},{6,4},{7,5},{8,10},{9,11},{10,... | collective-permute-start | bytes 1179656 | tf_op jit(solution)/shard_map/ppermute | solution.py:76
  54.9 13.2 %collective-permute-start.7 = (bf16[256,768]{1,0:T(8,128)(2,1)S(1)}, bf16[256,768]{1,0:T(8,128)(2,1)S(1)}, u32[]{:S(2)}, u32[]{:S(2)}) collective-permute-start(bf16[256,768]{1,0:T(8,128)(2,1)S(1)} %collective-permute-done.3), channel_id=1, source_target_pairs={{0,4},{1,5},{2,6},{3,7},{4,8},{5,9},{6,10},{7,11},{8,12},{9,13},{1... | collective-permute-start | bytes 1179656 | tf_op jit(solution)/shard_map/ppermute | solution.py:76
  54.9 22.2 %collective-permute-start.8 = (bf16[256,768]{1,0:T(8,128)(2,1)S(1)}, bf16[256,768]{1,0:T(8,128)(2,1)S(1)}, u32[]{:S(2)}, u32[]{:S(2)}) collective-permute-start(bf16[256,768]{1,0:T(8,128)(2,1)S(1)} %collective-permute-done.4), channel_id=1, source_target_pairs={{0,4},{1,5},{2,6},{3,7},{4,8},{5,9},{6,10},{7,11},{8,12},{9,13},{1... | collective-permute-start | bytes 1179656 | tf_op jit(solution)/shard_map/ppermute | solution.py:76
  55.0 29.4 %collective-permute-start.12 = (bf16[512,768]{1,0:T(8,128)(2,1)S(1)}, bf16[512,768]{1,0:T(8,128)(2,1)S(1)}, u32[]{:S(2)}, u32[]{:S(2)}) collective-permute-start(bf16[512,768]{1,0:T(8,128)(2,1)S(1)} %constant_dynamic-update-slice_fusion.6), channel_id=1, source_target_pairs={{0,1},{1,0},{2,3},{3,2},{4,5},{5,4},{6,7},{7,6},{8,9},{9,8},{10,11... | collective-permute-start | bytes 2359304 | tf_op jit(solution)/shard_map/ppermute | solution.py:76
  68.0 18.6 %collective-permute-start.2 = (bf16[512,768]{1,0:T(8,128)(2,1)}, bf16[512,768]{1,0:T(8,128)(2,1)S(1)}, u32[]{:S(2)}, u32[]{:S(2)}) collective-permute-start(bf16[512,768]{1,0:T(8,128)(2,1)} %collective-permute-done.1), channel_id=1, source_target_pairs={{0,1},{1,0},{2,3},{3,2},{4,5},{5,4},{6,7},{7,6},{8,9},{9,8},{10,11... | collective-permute-start | bytes 2359304 | tf_op jit(solution)/shard_map/ppermute | solution.py:76
  85.2 15.2 %collective-permute-start.18 = (f32[512]{0:T(512)S(1)}, f32[512]{0:T(512)S(1)}, u32[]{:S(2)}, u32[]{:S(2)}) collective-permute-start(f32[512]{0:T(512)S(1)} %maximum_maximum_fusion.1), channel_id=1, source_target_pairs={{0,250},{1,251},{2,248},{3,249},{4,254},{5,255},{6,252},{7,253},{8... | collective-permute-start | bytes 6152 | tf_op jit(solution)/shard_map/ppermute | solution.py:76
  86.0 9.1 %collective-permute-start.13 = (f32[4,512]{1,0:T(4,128)S(1)}, f32[4,512]{1,0:T(4,128)S(1)}, u32[]{:S(2)}, u32[]{:S(2)}) collective-permute-start(f32[4,512]{1,0:T(4,128)S(1)} %pad_maximum_fusion), channel_id=1, source_target_pairs={{0,4},{1,5},{2,6},{3,7},{4,8},{5,9},{6,10},{7,11},{8,12},{9,13},{1... | collective-permute-start | bytes 24584 | tf_op jit(solution)/shard_map/ppermute | solution.py:76
  87.3 13.0 %collective-permute-start.17 = (f32[512]{0:T(512)S(1)}, f32[512]{0:T(512)S(1)}, u32[]{:S(2)}, u32[]{:S(2)}) collective-permute-start(f32[512]{0:T(512)S(1)} %maximum_maximum_fusion.3), channel_id=1, source_target_pairs={{0,254},{1,255},{2,252},{3,253},{4,0},{5,1},{6,2},{7,3},{8,4},{9,5... | collective-permute-start | bytes 6152 | tf_op jit(solution)/shard_map/ppermute | solution.py:76
  95.1 5.8 %collective-permute-start.16 = (f32[512]{0:T(512)S(1)}, f32[512]{0:T(512)S(1)}, u32[]{:S(2)}, u32[]{:S(2)}) collective-permute-start(f32[512]{0:T(512)S(1)} %bitcast.61), channel_id=1, source_target_pairs={{0,1},{1,0},{2,3},{3,2},{4,5},{5,4},{6,7},{7,6},{8,9},{9,8},{10,11... | collective-permute-start | bytes 6152 | tf_op jit(solution)/shard_map/ppermute | solution.py:76
  98.9 3.0 %collective-permute-start.15 = (f32[512]{0:T(512)S(1)}, f32[512]{0:T(512)S(1)}, u32[]{:S(2)}, u32[]{:S(2)}) collective-permute-start(f32[512]{0:T(512)S(1)} %bitcast.60), channel_id=1, source_target_pairs={{0,3},{1,2},{2,1},{3,0},{4,7},{5,6},{6,5},{7,4},{8,11},{9,10},{10,... | collective-permute-start | bytes 6152 | tf_op jit(solution)/shard_map/ppermute | solution.py:76
  98.9 3.0 %collective-permute-start.14 = (f32[512]{0:T(512)S(1)}, f32[512]{0:T(512)S(1)}, u32[]{:S(2)}, u32[]{:S(2)}) collective-permute-start(f32[512]{0:T(512)S(1)} %bitcast.59), channel_id=1, source_target_pairs={{0,2},{1,3},{2,0},{3,1},{4,6},{5,7},{6,4},{7,5},{8,10},{9,11},{10,... | collective-permute-start | bytes 6152 | tf_op jit(solution)/shard_map/ppermute | solution.py:76

commit v2 on v1

--- a/solution.py
+++ b/solution.py
@@ -48,16 +48,6 @@
     return jnp.max(kept, axis=1), jnp.max(kept, axis=0)
 
 
-def own_pair(own, own_rank, peer, peer_rank):
-    earlier = jnp.where(
-        peer_rank[None, :] < own_rank[:, None], scores_of(own, peer), jnp.float32(LOW)
-    )
-    later = jnp.where(
-        own_rank[None, :] < peer_rank[:, None], scores_of(peer, own), jnp.float32(LOW)
-    )
-    return jnp.max(earlier, axis=1), jnp.max(later, axis=0)
-
-
 def largest(values):
     best = values[0]
     for value in values[1:]:
@@ -79,14 +69,18 @@
         start = (block_id * 4 + place_id) * rows
         return lax.dynamic_slice_in_dim(ranks, start, rows)
 
-    squares = jnp.sum(embeddings * embeddings, axis=1, keepdims=True)
-    unit = (embeddings * lax.rsqrt(squares + 1e-06)).astype(jnp.bfloat16)
+    def normalised(values):
+        squares = jnp.sum(values * values, axis=1, keepdims=True)
+        return (values * lax.rsqrt(squares + 1e-06)).astype(jnp.bfloat16)
+
+    halves = [normalised(half) for half in jnp.split(embeddings, 2)]
+    unit = jnp.concatenate(halves)
 
     def pieces(values, move):
         return [send(value, move) for value in values]
 
-    ups = pieces(jnp.split(unit, [256]), onward)
-    downs = pieces(jnp.split(unit, [256]), back)
+    ups = pieces(halves, onward)
+    downs = pieces(halves, back)
     across = send(unit, other(2))
     beside = send(unit, other(1))
     upps = pieces(ups, onward)
@@ -118,24 +112,20 @@
             out.append(pair(left[k], left_ranks[k], right, right_rank))
         return out
 
-    own = []
-    for k in range(4):
-        own.append(own_pair(unit, host_ranks[0], host[k], host_ranks[k]))
-    earlier = largest([pair[0] for pair in own])
-    later = largest([pair[1] for pair in own])
-
+    own = tiles(best_pair, host, host_ranks, unit, host_ranks[0])
     one = tiles(best_pair, host, host_ranks, visit1, rank1)
     two = tiles(best_pair, front, front_ranks, visit1, rank1)
     columns1 = largest([pair[1] for pair in one + two])
     three = tiles(best_pair, front, front_ranks, visit2, rank2)
     columns2 = largest([pair[1] for pair in three])
     front_rows = jnp.stack([jnp.maximum(a[0], b[0]) for a, b in zip(two, three)])
-    host_rows = jnp.stack([pair[0] for pair in one])
+    host_rows = jnp.stack([jnp.maximum(a[0], b[0]) for a, b in zip(own, one)])
 
     merged = jnp.maximum(host_rows, send(front_rows, onward))
+    later = largest([pair[1] for pair in own])
     later = jnp.maximum(later, send(columns1, back))
     later = jnp.maximum(later, send(columns2, back_twice))
-    earlier = jnp.maximum(earlier, merged[0])
+    earlier = merged[0]
     for k in (2, 3, 1):
         earlier = jnp.maximum(earlier, send(merged[k], other(k)))
     return earlier, later

time: 103 us -> 86.7 us (0.84)
  waiting for transfers between devices: 39.8 us -> 29.1 us
  matrix products: 16.3 us -> 13.3 us
  starting transfers between devices: 41.2 us -> 38.7 us
    ppermute x19, waiting for transfers between devices: 39.8 us -> 29.1 us  [send(): return lax.ppermute(value, AXES, routes(blocks, move))]
    dot_general x19 -> x16, matrix products: 16.3 us -> 13.3 us  [scores_of(): lax.dot_general(left, right, (((1,), (1,)), ((), ())), preferred_element_...]
    ppermute x19, starting transfers between devices: 41.2 us -> 38.7 us  [send(): return lax.ppermute(value, AXES, routes(blocks, move))]
where the time goes in v2:
time: 86.7 us; the launch traced here: 86.5 us
  starting transfers between devices  38.7 us (45%)
  waiting for transfers between devices  29.1 us (34%)
  matrix products  13.3 us (15%)
  other arithmetic  3.13 us (4%)
  local copies, waits for them, and re-layouts  1.35 us (2%)
  between operations  0.96 us (1%)
    ppermute x19, starting transfers between devices, send(): return lax.ppermute(value, AXES, routes(blocks, move))  38.7 us
    ppermute x19, waiting for transfers between devices, send(): return lax.ppermute(value, AXES, routes(blocks, move))  29.1 us
    dot_general x16, matrix products, scores_of(): lax.dot_general(left, right, (((1,), (1,)), ((), ())), preferred_element_...  13.3 us
  transfers between devices with their start and end apart: 19, of which 6 were waited for; matrix products, arithmetic and copies ran while one was open for 18% of the time, Pallas kernels for 0%

profile of v2, /device:TPU:1, one launch (start us, length us, event | category | flops | bytes accessed | tf_op | source)
XLA Modules:
  0.0 86.5 jit_solution(16906179411584548577)
XLA Ops:
  0.6 0.0 copy-start
  0.6 1.7 %multiply_reduce_fusion = (f32[256]{0:T(256)S(1)}, f32[256]{0:T(256)S(1)}) fusion(f32[512,768]{1,0:T(8,128)} %param.2), kind=kLoop, calls=%fused_computation.18 | loop fusion | flops 785920 | bytes 1574912 | tf_op jit(solution)/shard_map/reduce_sum | solution.py:73
  2.3 0.2 copy-done
  2.5 0.1 multiply_convert_fusion
  2.7 11.1 %collective-permute-start.5 = (bf16[256,768]{1,0:T(8,128)(2,1)S(1)}, bf16[256,768]{1,0:T(8,128)(2,1)S(1)}, u32[]{:S(2)}, u32[]{:S(2)}) collective-permute-start(bf16[256,768]{1,0:T(8,128)(2,1)S(1)} %get-tuple-element.37), channel_id=1, source_target_pairs={{0,254},{1,255},{2,252},{3,253},{4,0},{5,1},{6,2},{7,3},{8,4},{9,5... | collective-permute-start | bytes 1179656 | tf_op jit(solution)/shard_map/ppermute | solution.py:66
  13.8 0.0 collective-permute-start
  13.8 6.9 %collective-permute-start.6 = (bf16[256,768]{1,0:T(8,128)(2,1)S(1)}, bf16[256,768]{1,0:T(8,128)(2,1)S(1)}, u32[]{:S(2)}, u32[]{:S(2)}) collective-permute-start(bf16[256,768]{1,0:T(8,128)(2,1)S(1)} %get-tuple-element.36), channel_id=1, source_target_pairs={{0,254},{1,255},{2,252},{3,253},{4,0},{5,1},{6,2},{7,3},{8,4},{9,5... | collective-permute-start | bytes 1179656 | tf_op jit(solution)/shard_map/ppermute | solution.py:66
  20.7 0.0 collective-permute-start.1
  20.7 0.1 pad_maximum_fusion
  20.7 0.1 collective-permute-start.3
  20.9 0.9 %fusion.16 = (s32[512]{0:T(512)S(1)}, s32[512]{0:T(512)S(1)}, s32[512]{0:T(512)S(1)}, s32[512]{0:T(512)S(1)}, s32[512]{0:T(512)S(1)}, /*index=5*/s32[512]{0:T(51...) fusion(s32[131072]{0:T(1024)} %param.3, s32[]{:T(128)S(6)} %select_n.114, s32[]{:T(128)S(6)} %select_n.131, ...), kind=kLoop, calls=%fused_computation.53 | loop fusion | bytes 41000 | tf_op jit(solution)/shard_map/dynamic_slice | solution.py:70
  21.9 0.7 fusion.1
  22.6 0.0 collective-permute-done.5
  22.6 1.4 %collective-permute-start.10 = (bf16[256,768]{1,0:T(8,128)(2,1)S(1)}, bf16[256,768]{1,0:T(8,128)(2,1)S(1)}, u32[]{:S(2)}, u32[]{:S(2)}) collective-permute-start(bf16[256,768]{1,0:T(8,128)(2,1)S(1)} %collective-permute-done.5), channel_id=1, source_target_pairs={{0,2},{1,3},{2,0},{3,1},{4,6},{5,7},{6,4},{7,5},{8,10},{9,11},{10,... | collective-permute-start | bytes 1179656 | tf_op jit(solution)/shard_map/ppermute | solution.py:66
  24.0 6.0 %collective-permute-done.6 = bf16[256,768]{1,0:T(8,128)(2,1)S(1)} collective-permute-done((bf16[256,768]{1,0:T(8,128)(2,1)S(1)}, bf16[256,768]{1,0:T(8,128)(2,1)S(1)}, u32[]{:S(2)}, u32[]{:S(2)}) %collective-permute-start.6) | collective-permute-done | bytes 393248 | tf_op jit(solution)/shard_map/ppermute | solution.py:66
  30.0 0.0 collective-permute-start.11
  30.0 0.0 collective-permute-done
  30.1 7.2 %collective-permute-done.1 = bf16[256,768]{1,0:T(8,128)(2,1)S(1)} collective-permute-done((bf16[256,768]{1,0:T(8,128)(2,1)S(1)}, bf16[256,768]{1,0:T(8,128)(2,1)S(1)}, u32[]{:S(2)}, u32[]{:S(2)}) %collective-permute-start.1) | collective-permute-done | bytes 393248 | tf_op jit(solution)/shard_map/ppermute | solution.py:66
  37.4 0.7 fusion.8
  38.1 0.1 collective-permute-start.7
  38.2 0.1 collective-permute-start.8
  38.3 0.7 fusion.5
  39.0 7.9 %collective-permute-done.10 = bf16[256,768]{1,0:T(8,128)(2,1)S(1)} collective-permute-done((bf16[256,768]{1,0:T(8,128)(2,1)S(1)}, bf16[256,768]{1,0:T(8,128)(2,1)S(1)}, u32[]{:S(2)}, u32[]{:S(2)}) %collective-permute-start.10) | collective-permute-done | bytes 393248 | tf_op jit(solution)/shard_map/ppermute | solution.py:66
  46.8 4.3 %collective-permute-start.2 = (bf16[512,768]{1,0:T(8,128)(2,1)S(1)}, bf16[512,768]{1,0:T(8,128)(2,1)S(1)}, u32[]{:S(2)}, u32[]{:S(2)}) collective-permute-start(bf16[512,768]{1,0:T(8,128)(2,1)S(1)} %pad_maximum_fusion), channel_id=1, source_target_pairs={{0,1},{1,0},{2,3},{3,2},{4,5},{5,4},{6,7},{7,6},{8,9},{9,8},{10,11... | collective-permute-start | bytes 2359304 | tf_op jit(solution)/shard_map/ppermute | solution.py:66
  51.2 4.0 %collective-permute-done.11 = bf16[256,768]{1,0:T(8,128)(2,1)S(1)} collective-permute-done((bf16[256,768]{1,0:T(8,128)(2,1)S(1)}, bf16[256,768]{1,0:T(8,128)(2,1)S(1)}, u32[]{:S(2)}, u32[]{:S(2)}) %collective-permute-start.11) | collective-permute-done | bytes 393248 | tf_op jit(solution)/shard_map/ppermute | solution.py:66
  55.3 2.4 %collective-permute-start.9 = (bf16[512,768]{1,0:T(8,128)(2,1)S(1)}, bf16[512,768]{1,0:T(8,128)(2,1)S(1)}, u32[]{:S(2)}, u32[]{:S(2)}) collective-permute-start(bf16[512,768]{1,0:T(8,128)(2,1)S(1)} %constant_dynamic-update-slice_fusion.2), channel_id=1, source_target_pairs={{0,1},{1,0},{2,3},{3,2},{4,5},{5,4},{6,7},{7,6},{8,9},{9,8},{10,11... | collective-permute-start | bytes 2359304 | tf_op jit(solution)/shard_map/ppermute | solution.py:66
  57.7 0.0 collective-permute-done.7
  57.7 0.3 collective-permute-start.12
  58.0 2.9 %collective-permute-done.8 = bf16[256,768]{1,0:T(8,128)(2,1)S(1)} collective-permute-done((bf16[256,768]{1,0:T(8,128)(2,1)S(1)}, bf16[256,768]{1,0:T(8,128)(2,1)S(1)}, u32[]{:S(2)}, u32[]{:S(2)}) %collective-permute-start.8) | collective-permute-done | bytes 393248 | tf_op jit(solution)/shard_map/ppermute | solution.py:66
  60.9 0.7 fusion.10
  61.6 0.7 fusion.14
  62.3 0.7 fusion.13
  63.0 0.0 collective-permute-done.3
  63.0 1.8 %fusion.2 = (f32[512]{0:T(512)S(1)}, f32[512]{0:T(512)S(1)}) fusion(bf16[512,768]{1,0:T(8,128)(2,1)} %collective-permute-done.3, bf16[256,768]{1,0:T(8,128)(2,1)S(1)} %get-tuple-element.36, bf16[256,768]{1,0:T(8,128)(2,1)S(1)} %get-tuple-element.37, s32[512]{0:T(512)S(1)} %get-tuple-element.43, s32[512]{0:T(512)S(1)} %get-tuple-element.45), kind=kOutput, calls=%fused_computation.39 | convolution fusion | flops 405273600 | bytes 1581056 | tf_op jit(solution)/shard_map/dot_general | solution.py:39
  64.8 1.8 %fusion.6 = (f32[512]{0:T(512)S(1)}, f32[512]{0:T(512)S(1)}) fusion(bf16[512,768]{1,0:T(8,128)(2,1)} %collective-permute-done.3, bf16[512,768]{1,0:T(8,128)(2,1)S(1)} %constant_dynamic-update-slice_fusion, s32[512]{0:T(512)S(1)} %get-tuple-element.43, s32[512]{0:T(512)S(1)} %get-tuple-element.44), kind=kOutput, calls=%fused_computation.43 | convolution fusion | flops 403700736 | bytes 1581056 | tf_op jit(solution)/shard_map/dot_general | solution.py:39
  66.6 0.0 collective-permute-done.2
  66.6 0.7 fusion
  67.4 0.7 fusion.4
  68.1 2.7 %collective-permute-start.4 = (bf16[512,768]{1,0:T(8,128)(2,1)}, bf16[512,768]{1,0:T(8,128)(2,1)S(1)}, u32[]{:S(2)}, u32[]{:S(2)}) collective-permute-start(bf16[512,768]{1,0:T(8,128)(2,1)} %collective-permute-done.3), channel_id=1, source_target_pairs={{0,1},{1,0},{2,3},{3,2},{4,5},{5,4},{6,7},{7,6},{8,9},{9,8},{10,11... | collective-permute-start | bytes 2359304 | tf_op jit(solution)/shard_map/ppermute | solution.py:66
  70.8 0.0 collective-permute-done.9
  70.8 0.7 fusion.9
  71.5 0.7 fusion.12
  72.2 0.0 collective-permute-done.12
  72.2 0.7 fusion.11
  72.9 0.7 fusion.15
  73.6 0.1 collective-permute-start.13
  73.7 3.0 %collective-permute-start.18 = (f32[512]{0:T(512)S(1)}, f32[512]{0:T(512)S(1)}, u32[]{:S(2)}, u32[]{:S(2)}) collective-permute-start(f32[512]{0:T(512)S(1)} %maximum_maximum_fusion.1), channel_id=1, source_target_pairs={{0,250},{1,251},{2,248},{3,249},{4,254},{5,255},{6,252},{7,253},{8... | collective-permute-start | bytes 6152 | tf_op jit(solution)/shard_map/ppermute | solution.py:66
  76.7 0.0 collective-permute-done.4
  76.7 0.7 fusion.7
  77.4 4.0 %collective-permute-start.17 = (f32[512]{0:T(512)S(1)}, f32[512]{0:T(512)S(1)}, u32[]{:S(2)}, u32[]{:S(2)}) collective-permute-start(f32[512]{0:T(512)S(1)} %maximum_maximum_fusion.3), channel_id=1, source_target_pairs={{0,254},{1,255},{2,252},{3,253},{4,0},{5,1},{6,2},{7,3},{8,4},{9,5... | collective-permute-start | bytes 6152 | tf_op jit(solution)/shard_map/ppermute | solution.py:66
  81.4 0.7 fusion.3
  82.1 0.0 collective-permute-done.13
  82.1 0.8 collective-permute-start.16
  82.9 0.0 collective-permute-start.15
  82.9 1.4 %collective-permute-start.14 = (f32[512]{0:T(512)S(1)}, f32[512]{0:T(512)S(1)}, u32[]{:S(2)}, u32[]{:S(2)}) collective-permute-start(f32[512]{0:T(512)S(1)} %bitcast.47), channel_id=1, source_target_pairs={{0,2},{1,3},{2,0},{3,1},{4,6},{5,7},{6,4},{7,5},{8,10},{9,11},{10,... | collective-permute-start | bytes 6152 | tf_op jit(solution)/shard_map/ppermute | solution.py:66
  84.4 0.0 collective-permute-done.18
  84.4 0.0 collective-permute-done.17
  84.4 0.6 maximum_maximum_fusion.2
  85.0 0.0 collective-permute-done.16
  85.0 1.0 %collective-permute-done.15 = f32[512]{0:T(512)S(1)} collective-permute-done((f32[512]{0:T(512)S(1)}, f32[512]{0:T(512)S(1)}, u32[]{:S(2)}, u32[]{:S(2)}) %collective-permute-start.15) | collective-permute-done | bytes 2080 | tf_op jit(solution)/shard_map/ppermute | solution.py:66
  85.9 0.0 collective-permute-done.14
  85.9 0.6 maximum_maximum_fusion.4
  (22 shorter events, 0.3 us)
Async XLA Ops:
  0.6 1.9 %copy-start = (f32[512,768]{1,0:T(8,128)S(1)}, f32[512,768]{1,0:T(8,128)}, u32[]{:S(2)}) copy-start(f32[512,768]{1,0:T(8,128)} %param.2) | copy-start | bytes 4718596
  2.7 19.9 %collective-permute-start.5 = (bf16[256,768]{1,0:T(8,128)(2,1)S(1)}, bf16[256,768]{1,0:T(8,128)(2,1)S(1)}, u32[]{:S(2)}, u32[]{:S(2)}) collective-permute-start(bf16[256,768]{1,0:T(8,128)(2,1)S(1)} %get-tuple-element.37), channel_id=1, source_target_pairs={{0,254},{1,255},{2,252},{3,253},{4,0},{5,1},{6,2},{7,3},{8,4},{9,5... | collective-permute-start | bytes 1179656 | tf_op jit(solution)/shard_map/ppermute | solution.py:66
  13.8 16.3 %collective-permute-start = (bf16[256,768]{1,0:T(8,128)(2,1)S(1)}, bf16[256,768]{1,0:T(8,128)(2,1)S(1)}, u32[]{:S(2)}, u32[]{:S(2)}) collective-permute-start(bf16[256,768]{1,0:T(8,128)(2,1)S(1)} %get-tuple-element.37), channel_id=1, source_target_pairs={{0,4},{1,5},{2,6},{3,7},{4,8},{5,9},{6,10},{7,11},{8,12},{9,13},{1... | collective-permute-start | bytes 1179656 | tf_op jit(solution)/shard_map/ppermute | solution.py:66
  13.8 16.2 %collective-permute-start.6 = (bf16[256,768]{1,0:T(8,128)(2,1)S(1)}, bf16[256,768]{1,0:T(8,128)(2,1)S(1)}, u32[]{:S(2)}, u32[]{:S(2)}) collective-permute-start(bf16[256,768]{1,0:T(8,128)(2,1)S(1)} %get-tuple-element.36), channel_id=1, source_target_pairs={{0,254},{1,255},{2,252},{3,253},{4,0},{5,1},{6,2},{7,3},{8,4},{9,5... | collective-permute-start | bytes 1179656 | tf_op jit(solution)/shard_map/ppermute | solution.py:66
  20.7 16.7 %collective-permute-start.1 = (bf16[256,768]{1,0:T(8,128)(2,1)S(1)}, bf16[256,768]{1,0:T(8,128)(2,1)S(1)}, u32[]{:S(2)}, u32[]{:S(2)}) collective-permute-start(bf16[256,768]{1,0:T(8,128)(2,1)S(1)} %get-tuple-element.36), channel_id=1, source_target_pairs={{0,4},{1,5},{2,6},{3,7},{4,8},{5,9},{6,10},{7,11},{8,12},{9,13},{1... | collective-permute-start | bytes 1179656 | tf_op jit(solution)/shard_map/ppermute | solution.py:66
  20.7 42.2 %collective-permute-start.3 = (bf16[512,768]{1,0:T(8,128)(2,1)S(1)}, bf16[512,768]{1,0:T(8,128)(2,1)}, u32[]{:S(2)}, u32[]{:S(2)}) collective-permute-start(bf16[512,768]{1,0:T(8,128)(2,1)S(1)} %pad_maximum_fusion), channel_id=1, source_target_pairs={{0,2},{1,3},{2,0},{3,1},{4,6},{5,7},{6,4},{7,5},{8,10},{9,11},{10,... | collective-permute-start | bytes 2359304 | tf_op jit(solution)/shard_map/ppermute | solution.py:66
  22.6 24.3 %collective-permute-start.10 = (bf16[256,768]{1,0:T(8,128)(2,1)S(1)}, bf16[256,768]{1,0:T(8,128)(2,1)S(1)}, u32[]{:S(2)}, u32[]{:S(2)}) collective-permute-start(bf16[256,768]{1,0:T(8,128)(2,1)S(1)} %collective-permute-done.5), channel_id=1, source_target_pairs={{0,2},{1,3},{2,0},{3,1},{4,6},{5,7},{6,4},{7,5},{8,10},{9,11},{10,... | collective-permute-start | bytes 1179656 | tf_op jit(solution)/shard_map/ppermute | solution.py:66
  30.0 25.2 %collective-permute-start.11 = (bf16[256,768]{1,0:T(8,128)(2,1)S(1)}, bf16[256,768]{1,0:T(8,128)(2,1)S(1)}, u32[]{:S(2)}, u32[]{:S(2)}) collective-permute-start(bf16[256,768]{1,0:T(8,128)(2,1)S(1)} %collective-permute-done.6), channel_id=1, source_target_pairs={{0,2},{1,3},{2,0},{3,1},{4,6},{5,7},{6,4},{7,5},{8,10},{9,11},{10,... | collective-permute-start | bytes 1179656 | tf_op jit(solution)/shard_map/ppermute | solution.py:66
  38.1 19.6 %collective-permute-start.7 = (bf16[256,768]{1,0:T(8,128)(2,1)S(1)}, bf16[256,768]{1,0:T(8,128)(2,1)S(1)}, u32[]{:S(2)}, u32[]{:S(2)}) collective-permute-start(bf16[256,768]{1,0:T(8,128)(2,1)S(1)} %collective-permute-done), channel_id=1, source_target_pairs={{0,4},{1,5},{2,6},{3,7},{4,8},{5,9},{6,10},{7,11},{8,12},{9,13},{1... | collective-permute-start | bytes 1179656 | tf_op jit(solution)/shard_map/ppermute | solution.py:66
  38.2 22.7 %collective-permute-start.8 = (bf16[256,768]{1,0:T(8,128)(2,1)S(1)}, bf16[256,768]{1,0:T(8,128)(2,1)S(1)}, u32[]{:S(2)}, u32[]{:S(2)}) collective-permute-start(bf16[256,768]{1,0:T(8,128)(2,1)S(1)} %collective-permute-done.1), channel_id=1, source_target_pairs={{0,4},{1,5},{2,6},{3,7},{4,8},{5,9},{6,10},{7,11},{8,12},{9,13},{1... | collective-permute-start | bytes 1179656 | tf_op jit(solution)/shard_map/ppermute | solution.py:66
  46.8 19.8 %collective-permute-start.2 = (bf16[512,768]{1,0:T(8,128)(2,1)S(1)}, bf16[512,768]{1,0:T(8,128)(2,1)S(1)}, u32[]{:S(2)}, u32[]{:S(2)}) collective-permute-start(bf16[512,768]{1,0:T(8,128)(2,1)S(1)} %pad_maximum_fusion), channel_id=1, source_target_pairs={{0,1},{1,0},{2,3},{3,2},{4,5},{5,4},{6,7},{7,6},{8,9},{9,8},{10,11... | collective-permute-start | bytes 2359304 | tf_op jit(solution)/shard_map/ppermute | solution.py:66
  55.3 15.5 %collective-permute-start.9 = (bf16[512,768]{1,0:T(8,128)(2,1)S(1)}, bf16[512,768]{1,0:T(8,128)(2,1)S(1)}, u32[]{:S(2)}, u32[]{:S(2)}) collective-permute-start(bf16[512,768]{1,0:T(8,128)(2,1)S(1)} %constant_dynamic-update-slice_fusion.2), channel_id=1, source_target_pairs={{0,1},{1,0},{2,3},{3,2},{4,5},{5,4},{6,7},{7,6},{8,9},{9,8},{10,11... | collective-permute-start | bytes 2359304 | tf_op jit(solution)/shard_map/ppermute | solution.py:66
  57.7 14.5 %collective-permute-start.12 = (bf16[512,768]{1,0:T(8,128)(2,1)S(1)}, bf16[512,768]{1,0:T(8,128)(2,1)S(1)}, u32[]{:S(2)}, u32[]{:S(2)}) collective-permute-start(bf16[512,768]{1,0:T(8,128)(2,1)S(1)} %constant_dynamic-update-slice_fusion.6), channel_id=1, source_target_pairs={{0,1},{1,0},{2,3},{3,2},{4,5},{5,4},{6,7},{7,6},{8,9},{9,8},{10,11... | collective-permute-start | bytes 2359304 | tf_op jit(solution)/shard_map/ppermute | solution.py:66
  68.1 8.7 %collective-permute-start.4 = (bf16[512,768]{1,0:T(8,128)(2,1)}, bf16[512,768]{1,0:T(8,128)(2,1)S(1)}, u32[]{:S(2)}, u32[]{:S(2)}) collective-permute-start(bf16[512,768]{1,0:T(8,128)(2,1)} %collective-permute-done.3), channel_id=1, source_target_pairs={{0,1},{1,0},{2,3},{3,2},{4,5},{5,4},{6,7},{7,6},{8,9},{9,8},{10,11... | collective-permute-start | bytes 2359304 | tf_op jit(solution)/shard_map/ppermute | solution.py:66
  73.6 8.5 %collective-permute-start.13 = (f32[4,512]{1,0:T(4,128)S(1)}, f32[4,512]{1,0:T(4,128)S(1)}, u32[]{:S(2)}, u32[]{:S(2)}) collective-permute-start(f32[4,512]{1,0:T(4,128)S(1)} %pad_maximum_fusion.1), channel_id=1, source_target_pairs={{0,4},{1,5},{2,6},{3,7},{4,8},{5,9},{6,10},{7,11},{8,12},{9,13},{1... | collective-permute-start | bytes 24584 | tf_op jit(solution)/shard_map/ppermute | solution.py:66
  73.7 10.6 %collective-permute-start.18 = (f32[512]{0:T(512)S(1)}, f32[512]{0:T(512)S(1)}, u32[]{:S(2)}, u32[]{:S(2)}) collective-permute-start(f32[512]{0:T(512)S(1)} %maximum_maximum_fusion.1), channel_id=1, source_target_pairs={{0,250},{1,251},{2,248},{3,249},{4,254},{5,255},{6,252},{7,253},{8... | collective-permute-start | bytes 6152 | tf_op jit(solution)/shard_map/ppermute | solution.py:66
  77.4 6.9 %collective-permute-start.17 = (f32[512]{0:T(512)S(1)}, f32[512]{0:T(512)S(1)}, u32[]{:S(2)}, u32[]{:S(2)}) collective-permute-start(f32[512]{0:T(512)S(1)} %maximum_maximum_fusion.3), channel_id=1, source_target_pairs={{0,254},{1,255},{2,252},{3,253},{4,0},{5,1},{6,2},{7,3},{8,4},{9,5... | collective-permute-start | bytes 6152 | tf_op jit(solution)/shard_map/ppermute | solution.py:66
  82.1 2.8 %collective-permute-start.16 = (f32[512]{0:T(512)S(1)}, f32[512]{0:T(512)S(1)}, u32[]{:S(2)}, u32[]{:S(2)}) collective-permute-start(f32[512]{0:T(512)S(1)} %bitcast.49), channel_id=1, source_target_pairs={{0,1},{1,0},{2,3},{3,2},{4,5},{5,4},{6,7},{7,6},{8,9},{9,8},{10,11... | collective-permute-start | bytes 6152 | tf_op jit(solution)/shard_map/ppermute | solution.py:66
  82.9 3.0 %collective-permute-start.15 = (f32[512]{0:T(512)S(1)}, f32[512]{0:T(512)S(1)}, u32[]{:S(2)}, u32[]{:S(2)}) collective-permute-start(f32[512]{0:T(512)S(1)} %bitcast.48), channel_id=1, source_target_pairs={{0,3},{1,2},{2,1},{3,0},{4,7},{5,6},{6,5},{7,4},{8,11},{9,10},{10,... | collective-permute-start | bytes 6152 | tf_op jit(solution)/shard_map/ppermute | solution.py:66
  82.9 3.0 %collective-permute-start.14 = (f32[512]{0:T(512)S(1)}, f32[512]{0:T(512)S(1)}, u32[]{:S(2)}, u32[]{:S(2)}) collective-permute-start(f32[512]{0:T(512)S(1)} %bitcast.47), channel_id=1, source_target_pairs={{0,2},{1,3},{2,0},{3,1},{4,6},{5,7},{6,4},{7,5},{8,10},{9,11},{10,... | collective-permute-start | bytes 6152 | tf_op jit(solution)/shard_map/ppermute | solution.py:66
